TPU v7x, 32 devices: a whole 2x2x4 slice. The times are simulated.
32 devices in a mesh: tm: 16 (over z, x, core), freq: 2 (over y).
Axes of the slice: x: 2, y: 2, z: 4, core: 2. Of those that a mesh axis runs over, the one named last changes fastest.
Arguments:
- strengths: bfloat16 [2, 8, 256, 32768], P(None, 'freq', None, 'tm'), may hold values from -6 to 6
- sample_cell: int32 [32768], P('tm'), may hold values from 0 to 16383, as said below
- sample_frac: float32 [32768], P('tm'), may hold values from 0 to 1
Outputs:
- spectra: float32 [2, 8, 256, 4, 32, 128], P(None, None, 'tm', 'freq')
Inputs may be any that keep to these rules, and one draw needn't show every extreme that they name: `sample_cell`: the samples of the i-th aligned block of 2048 samples lie in cells i * 1024 to (i + 1) * 1024 - 1; in every block the first sample lies in the first of these cells and the second sample in the last.
All inputs are finite; a program needn't handle non-finite values.
Results may differ from a plain program's by a relative error of at most 0.0037.
Values may be sent and summed in bfloat16 or wider, within the bound.
A program may use at most 128 MiB of HBM per device.

v0:
```python
import math

import jax
import jax.numpy as jnp
import numpy as np
from jax import lax
from jax.experimental import pallas as pl
from jax.experimental.pallas import tpu as pltpu
from jax.sharding import PartitionSpec as P

TAPS = 8
HALF = TAPS // 2
GRID_DEV = 1024
FFT_LO = 32
FFT_HI = 128
FFTLEN = 4096
SHARP = 0.3
MESH = pl.DeviceIdType.MESH
SLABS = GRID_DEV // FFT_HI
PER_FRAME = FFTLEN // GRID_DEV


def tap_table(local_cell, fraction, columns):
    offset = columns[None, :] - local_cell[:, None] - 1
    inside = (offset >= 0) & (offset < TAPS)
    shifted = offset.astype(jnp.float32) - float(HALF - 1) - fraction[:, None]
    values = jnp.exp(-SHARP * (shifted * shifted))
    return jnp.where(inside, values, 0.0).astype(jnp.bfloat16)


def spread_kernel(s_ref, h_ref, w_ref, e_ref, o_ref):
    rows = s_ref.shape[0] * s_ref.shape[1] * s_ref.shape[2]
    s = s_ref[...].reshape(rows, s_ref.shape[3])
    h = h_ref[...].reshape(rows, h_ref.shape[3])
    acc = jnp.dot(s, w_ref[...], preferred_element_type=jnp.float32)
    acc = acc + jnp.dot(h, e_ref[...], preferred_element_type=jnp.float32)
    acc = acc.astype(jnp.bfloat16)
    for j in range(SLABS):
        o_ref[0, j] = acc[:, j * FFT_HI : (j + 1) * FFT_HI]


def spread(strengths, halo_cols, table, select, n_tm):
    parts, groups, channels, samples = strengths.shape
    chunk = channels // n_tm
    rows = parts * groups * chunk
    lanes = halo_cols.shape[3]
    return pl.pallas_call(
        spread_kernel,
        out_shape=jax.ShapeDtypeStruct((n_tm, SLABS, rows, FFT_HI), jnp.bfloat16),
        grid=(n_tm,),
        in_specs=[
            pl.BlockSpec((parts, groups, chunk, samples), lambda d: (0, 0, d, 0)),
            pl.BlockSpec((parts, groups, chunk, lanes), lambda d: (0, 0, d, 0)),
            pl.BlockSpec((samples, GRID_DEV), lambda d: (0, 0)),
            pl.BlockSpec((lanes, GRID_DEV), lambda d: (0, 0)),
        ],
        out_specs=pl.BlockSpec((1, SLABS, rows, FFT_HI), lambda d: (d, 0, 0, 0)),
        name="spread",
    )(strengths, halo_cols, table, select)


def exchange_kernel(n_tm, n_fq, src, out, send1, recv1, send2, recv2, local_sem):
    t = lax.axis_index("tm")
    f = lax.axis_index("freq")
    span = n_tm // n_fq
    slot = lax.rem(t, span)
    home = lax.div(t, span)
    barrier = pltpu.get_barrier_semaphore()

    def greet_tm(i, c):
        pl.semaphore_signal(barrier, inc=1, device_id=(lax.rem(t + i, n_tm), f), device_id_type=MESH)
        return c

    def greet_fq(i, c):
        pl.semaphore_signal(barrier, inc=1, device_id=(t, lax.rem(f + i, n_fq)), device_id_type=MESH)
        return c

    lax.fori_loop(1, n_tm, greet_tm, 0)
    lax.fori_loop(1, n_fq, greet_fq, 0)
    pl.semaphore_wait(barrier, n_tm - 1 + n_fq - 1)

    def place(target):
        return jnp.where(target == f, f, n_fq + target)

    def first(peer):
        return pltpu.make_async_remote_copy(
            src_ref=src.at[peer],
            dst_ref=out.at[place(home), slot],
            send_sem=send1.at[peer],
            recv_sem=recv1.at[t],
            device_id=(peer, f),
            device_id_type=MESH,
        )

    def first_landed(origin):
        return pltpu.make_async_remote_copy(
            src_ref=src.at[origin],
            dst_ref=out.at[place(lax.div(origin, span)), lax.rem(origin, span)],
            send_sem=send1.at[origin],
            recv_sem=recv1.at[origin],
            device_id=(origin, f),
            device_id_type=MESH,
        )

    def second(target, s):
        return pltpu.make_async_remote_copy(
            src_ref=out.at[n_fq + target, s],
            dst_ref=out.at[f, s],
            send_sem=send2.at[target, s],
            recv_sem=recv2.at[f, s],
            device_id=(t, target),
            device_id_type=MESH,
        )

    def second_landed(origin, s):
        return pltpu.make_async_remote_copy(
            src_ref=out.at[n_fq + origin, s],
            dst_ref=out.at[origin, s],
            send_sem=send2.at[origin, s],
            recv_sem=recv2.at[origin, s],
            device_id=(t, origin),
            device_id_type=MESH,
        )

    half = n_tm // 2
    upper = lax.div(t, half)

    def far(i, c):
        first((1 - upper) * half + lax.rem(t + i, half)).start()
        return c

    def near(i, c):
        first(upper * half + lax.rem(t + i, half)).start()
        return c

    lax.fori_loop(0, half, far, 0)
    lax.fori_loop(1, half, near, 0)
    own = pltpu.make_async_copy(src.at[t], out.at[place(home), slot], local_sem)
    own.start()
    own.wait()

    def relay_group(k, c):
        target = lax.rem(f + k, n_fq)

        def relay(i, c):
            s = lax.rem(slot + span - i, span)
            origin = target * span + s

            @pl.when(origin != t)
            def _():
                first_landed(origin).wait_recv()

            second(target, s).start()
            return c

        return lax.fori_loop(0, span, relay, c)

    lax.fori_loop(1, n_fq, relay_group, 0)

    def kept(s, c):
        origin = f * span + s

        @pl.when(origin != t)
        def _():
            first_landed(origin).wait_recv()

        return c

    lax.fori_loop(0, span, kept, 0)

    def finish_first(i, c):
        first(lax.rem(t + i, n_tm)).wait_send()
        return c

    lax.fori_loop(1, n_tm, finish_first, 0)

    def finish_group(k, c):
        other = lax.rem(f + k, n_fq)

        def finish(s, c):
            second(other, s).wait_send()
            second_landed(other, s).wait_recv()
            return c

        return lax.fori_loop(0, span, finish, c)

    lax.fori_loop(1, n_fq, finish_group, 0)


def exchange(blocks, n_tm, n_fq):
    import functools

    span = n_tm // n_fq
    return pl.pallas_call(
        functools.partial(exchange_kernel, n_tm, n_fq),
        out_shape=jax.ShapeDtypeStruct((2 * n_fq, span) + blocks.shape[1:], jnp.bfloat16),
        in_specs=[pl.BlockSpec(memory_space=pl.ANY)],
        out_specs=pl.BlockSpec(memory_space=pl.ANY),
        scratch_shapes=[
            pltpu.SemaphoreType.DMA((n_tm,)),
            pltpu.SemaphoreType.DMA((n_tm,)),
            pltpu.SemaphoreType.DMA((n_fq, span)),
            pltpu.SemaphoreType.DMA((n_fq, span)),
            pltpu.SemaphoreType.DMA,
        ],
        compiler_params=pltpu.CompilerParams(collective_id=0, has_side_effects=True),
        name="exchange",
    )(blocks)


def fft_list(re, im):
    n = len(re)
    if n == 1:
        return re, im
    er, ei = fft_list(re[0::2], im[0::2])
    orr, oi = fft_list(re[1::2], im[1::2])
    out_r, out_i = [None] * n, [None] * n
    for k in range(n // 2):
        c, s = math.cos(2 * math.pi * k / n), math.sin(2 * math.pi * k / n)
        a, b = orr[k], oi[k]
        if k == 0:
            tr, ti = a, b
        elif 4 * k == n:
            tr, ti = b, -a
        elif 8 * k == n:
            tr, ti = (a + b) * c, (b - a) * c
        elif 8 * k == 3 * n:
            tr, ti = (b - a) * s, -(a + b) * s
        else:
            tr, ti = a * c + b * s, b * c - a * s
        out_r[k], out_i[k] = er[k] + tr, ei[k] + ti
        out_r[k + n // 2], out_i[k + n // 2] = er[k] - tr, ei[k] - ti
    return out_r, out_i


def transform_kernel(x_ref, tc_ref, ts_ref, hi_ref, lo_ref, o_ref, lhs, turned):
    chunk = x_ref.shape[5]
    re = [x_ref[0, n // SLABS, n % SLABS, 0, 0].astype(jnp.float32) for n in range(FFT_LO)]
    im = [x_ref[0, n // SLABS, n % SLABS, 1, 0].astype(jnp.float32) for n in range(FFT_LO)]
    re, im = fft_list(re, im)
    for a in range(FFT_LO):
        c = tc_ref[a : a + 1, :]
        s = ts_ref[a : a + 1, :]
        rows = pl.ds(a * chunk, chunk)
        lhs[rows, :FFT_HI] = (re[a] * c + im[a] * s).astype(jnp.bfloat16)
        lhs[rows, FFT_HI:] = (im[a] * c - re[a] * s).astype(jnp.bfloat16)
    x = lhs[...]
    y = jnp.dot(x, hi_ref[...], preferred_element_type=jnp.float32)
    y = y + jnp.dot(x, lo_ref[...], preferred_element_type=jnp.float32)
    for p in range(2):
        for a in range(FFT_LO):
            turned[p, pl.ds(a, chunk, stride=FFT_LO), :] = y[
                a * chunk : (a + 1) * chunk, p * FFT_HI : (p + 1) * FFT_HI
            ]
        o_ref[p, 0, :, 0] = turned[p].reshape(chunk, FFT_LO, FFT_HI)


def transform(held, n_fq, groups, chunk, frames):
    span = held.shape[1]
    x = held.reshape(2 * n_fq, span, SLABS, 2, groups, chunk, FFT_HI)
    low = np.arange(FFT_LO)[:, None] * np.arange(FFT_HI)[None, :] * (2 * math.pi / FFTLEN)
    high = np.arange(FFT_HI)[:, None] * np.arange(FFT_HI)[None, :] % FFT_HI * (2 * math.pi / FFT_HI)
    hc, hs = np.cos(high), np.sin(high)
    full = np.block([[hc, -hs], [hs, hc]]).astype(np.float32) / math.sqrt(FFTLEN)
    hi = full.astype(jnp.bfloat16)
    lo = (full - hi.astype(np.float32)).astype(jnp.bfloat16)
    whole = lambda shape: pl.BlockSpec(shape, lambda f, g, m: (0, 0))
    return pl.pallas_call(
        transform_kernel,
        out_shape=jax.ShapeDtypeStruct(
            (2, n_fq * groups, chunk, frames, FFT_LO, FFT_HI), jnp.float32
        ),
        grid=(n_fq, groups, frames),
        in_specs=[
            pl.BlockSpec(
                (1, PER_FRAME, SLABS, 2, 1, chunk, FFT_HI), lambda f, g, m: (f, m, 0, 0, g, 0, 0)
            ),
            whole((FFT_LO, FFT_HI)),
            whole((FFT_LO, FFT_HI)),
            whole((2 * FFT_HI, 2 * FFT_HI)),
            whole((2 * FFT_HI, 2 * FFT_HI)),
        ],
        out_specs=pl.BlockSpec(
            (2, 1, chunk, 1, FFT_LO, FFT_HI), lambda f, g, m: (0, f * groups + g, 0, m, 0, 0)
        ),
        scratch_shapes=[
            pltpu.VMEM((FFT_LO * chunk, 2 * FFT_HI), jnp.bfloat16),
            pltpu.VMEM((2, FFT_LO * chunk, FFT_HI), jnp.float32),
        ],
        name="transform",
    )(
        x,
        jnp.asarray(np.cos(low), jnp.float32),
        jnp.asarray(np.sin(low), jnp.float32),
        jnp.asarray(hi),
        jnp.asarray(lo),
    )


def shards(strengths, sample_cell, sample_frac):
    n_tm, n_fq = lax.axis_size("tm"), lax.axis_size("freq")
    parts, groups, channels, samples = strengths.shape
    local_cell = sample_cell - lax.axis_index("tm") * GRID_DEV
    edge_columns = jnp.concatenate(
        [
            jnp.arange(HALF, dtype=jnp.int32),
            jnp.arange(GRID_DEV + HALF, GRID_DEV + TAPS, dtype=jnp.int32),
        ]
    )
    edge_table = tap_table(local_cell, sample_frac, edge_columns)
    edges = lax.dot_general(
        edge_table,
        strengths.reshape(parts * groups * channels, samples),
        (((0,), (1,)), ((), ())),
        preferred_element_type=jnp.float32,
    )
    from_left = lax.ppermute(edges[HALF:], "tm", [(i, (i + 1) % n_tm) for i in range(n_tm)])
    from_right = lax.ppermute(edges[:HALF], "tm", [((i + 1) % n_tm, i) for i in range(n_tm)])
    table = tap_table(local_cell, sample_frac, jnp.arange(HALF, HALF + GRID_DEV, dtype=jnp.int32))
    halo = jnp.concatenate([from_left, from_right], axis=0)
    h0 = lax.reduce_precision(halo, 8, 7)
    h1 = lax.reduce_precision(halo - h0, 8, 7)
    h2 = halo - h0 - h1
    split = jnp.concatenate([h0, h1, h2], axis=0)
    halo_cols = jnp.pad(split.T, ((0, 0), (0, 128 - 3 * TAPS))).astype(jnp.bfloat16)
    pick = np.zeros((128, GRID_DEV), np.float32)
    for r in range(3):
        for k in range(HALF):
            pick[r * TAPS + k, k] = 1.0
            pick[r * TAPS + HALF + k, GRID_DEV - HALF + k] = 1.0
    blocks = spread(
        strengths,
        halo_cols.reshape(parts, groups, channels, 128),
        table,
        jnp.asarray(pick, jnp.bfloat16),
        n_tm,
    )
    held = exchange(blocks, n_tm, n_fq)
    frames = n_tm // PER_FRAME // n_fq
    return transform(held, n_fq, groups, channels // n_tm, frames)


def solution(mesh):
    placed = (P(None, "freq", None, "tm"), P("tm"), P("tm"))
    return jax.shard_map(
        shards,
        mesh=mesh,
        in_specs=placed,
        out_specs=P(None, None, "tm", "freq", None, None),
        check_vma=False,
    )
```

profile of v0, /device:TPU:0, one launch (start us, length us, event | category | flops | bytes accessed | tf_op | source)
XLA Modules:
  0.0 161.0 jit_solution(5855998432749109670)
XLA Ops:
  0.0 0.0 copy-start
  0.0 0.1 pad_add_fusion
  0.1 0.7 broadcast_subtract_fusion
  0.8 5.7 %fusion.7 = f32[8,2048]{1,0:T(8,128)S(1)} fusion(bf16[2048,2048]{1,0:T(8,128)(2,1)} %bitcast.6, f32[2048]{0:T(1024)} %param.10, s32[2048]{0:T(1024)S(1)} %broadcast_subtract_fusion, s32[8]{0:T(128)S(1)} %pad_add_fusion), kind=kOutput, calls=%fused_computation.17 | convolution fusion | flops 67305472 | bytes 8470560 | tf_op jit(solution)/shard_map/dot_general | solution.py:311
  6.5 0.5 collective-permute-start
  7.0 5.0 %collective-permute-start.1 = (f32[4,2048]{1,0:T(4,128)S(1)}, f32[4,2048]{1,0:T(4,128)S(1)}, u32[]{:S(2)}, u32[]{:S(2)}) collective-permute-start(f32[4,2048]{1,0:T(4,128)S(1)} %get-tuple-element.9), channel_id=1, source_target_pairs={{2,0},{4,2},{6,4},{8,6},{10,8},{12,10},{14,12},{16,14},{18,16},{20... | collective-permute-start | bytes 98312 | tf_op jit(solution)/shard_map/ppermute | solution.py:318
  12.1 0.0 copy-done
  12.1 6.1 %select_convert_fusion.w_ref = bf16[2048,1024]{1,0:T(8,128)(2,1)} fusion(f32[2048]{0:T(1024)S(1)} %copy-done, s32[2048]{0:T(1024)S(1)} %broadcast_subtract_fusion, s32[1024]{0:T(1024)S(1)} %iota_add_fusion), kind=kLoop, calls=%fused_computation | loop fusion | flops 25165824 | bytes 4214784 | tf_op jit(solution)/shard_map/convert_element_type | solution.py:28
  18.2 0.0 collective-permute-done
  18.2 0.0 collective-permute-done.1
  18.2 0.3 copy.11
  18.5 0.9 pad.5.clone
  19.4 18.5 %spread.1.src = bf16[16,8,128,128]{3,2,1,0:T(8,128)(2,1)} custom-call(bf16[2,4,256,2048]{3,2,1,0:T(8,128)(2,1)} %s_ref.1, bf16[2,4,256,128]{3,2,1,0:T(8,128)(2,1)} %bitcast.8, bf16[2048,1024]{1,0:T(8,128)(2,1)} %select_convert_fusion.w_ref, bf16[128,1024]{1,0:T(8,128)(2,1)} %constant.47.clone.e_ref), custom_call_target="tpu_custom_call" | custom-call | tf_op jit(solution)/shard_map/spread/pallas_call | solution.py:47
  37.9 105.0 %exchange.1 = bf16[4,8,8,128,128]{4,3,2,1,0:T(8,128)(2,1)} custom-call(bf16[16,8,128,128]{3,2,1,0:T(8,128)(2,1)} %spread.1.src), custom_call_target="tpu_custom_call" | custom-call | tf_op jit(solution)/shard_map/exchange/pallas_call | solution.py:194
  142.9 18.2 %transform.1 = f32[2,8,16,2,32,128]{5,4,3,2,1,0:T(8,128)} custom-call(bf16[4,8,8,2,4,16,128]{6,5,4,3,2,1,0:T(8,128)(2,1)} %bitcast.7, f32[32,128]{1,0:T(8,128)} %constant.48.clone.tc_ref, f32[32,128]{1,0:T(8,128)} %constant.49.clone.ts_ref, bf16[256,256]{1,0:T(8,128)(2,1)} %constant.50.clone.hi_ref, bf16[256,256]{1,0:T(8,128)(2,1)} %constant.51.clone.lo_ref), custom_call_target="tpu_custom_call" | custom-call | tf_op jit(solution)/shard_map/transform/pallas_call | solution.py:268
  (6 shorter events, 0.1 us)
Async XLA Ops:
  0.0 12.1 %copy-start = (f32[2048]{0:T(1024)S(1)}, f32[2048]{0:T(1024)}, u32[]{:S(2)}) copy-start(f32[2048]{0:T(1024)} %param.10) | copy-start | bytes 24580
  6.5 11.7 %collective-permute-start = (f32[4,2048]{1,0:T(4,128)S(1)}, f32[4,2048]{1,0:T(4,128)S(1)}, u32[]{:S(2)}, u32[]{:S(2)}) collective-permute-start(f32[4,2048]{1,0:T(4,128)S(1)} %get-tuple-element.8), channel_id=1, source_target_pairs={{0,2},{2,4},{4,6},{6,8},{8,10},{10,12},{12,14},{14,16},{16,18},{18... | collective-permute-start | bytes 98312 | tf_op jit(solution)/shard_map/ppermute | solution.py:317
  7.0 11.2 %collective-permute-start.1 = (f32[4,2048]{1,0:T(4,128)S(1)}, f32[4,2048]{1,0:T(4,128)S(1)}, u32[]{:S(2)}, u32[]{:S(2)}) collective-permute-start(f32[4,2048]{1,0:T(4,128)S(1)} %get-tuple-element.9), channel_id=1, source_target_pairs={{2,0},{4,2},{6,4},{8,6},{10,8},{12,10},{14,12},{16,14},{18,16},{20... | collective-permute-start | bytes 98312 | tf_op jit(solution)/shard_map/ppermute | solution.py:318
where the time goes:
time: 162 us; the launch traced here: 161 us
  Pallas kernels  142 us (88%)
  other arithmetic  6.95 us (4%)
  matrix products  5.67 us (4%)
  starting transfers between devices  5.56 us (3%)
    pallas_call x1, Pallas kernels, exchange(): pl.pallas_call(functools.partial(exchange_kernel, n_tm, n_fq), out_shape=...  105 us
    pallas_call x1, Pallas kernels, spread(): pl.pallas_call(spread_kernel, out_shape=jax.ShapeDtypeStruct((n_tm, SLABS...  18.5 us
    pallas_call x1, Pallas kernels, transform(): pl.pallas_call(transform_kernel, out_shape=jax.ShapeDtypeStruct((2, n_fq...  18.2 us
    convert_element_type x1, other arithmetic, tap_table(): return jnp.where(inside, values, 0.0).astype(jnp.bfloat16)  6.13 us
    dot_general x1, matrix products, shards(): lax.dot_general(edge_table, strengths.reshape(parts * groups * channels,...  5.67 us
    ppermute x1, starting transfers between devices, shards(): lax.ppermute(edges[:HALF], 'tm', [((i + 1) % n_tm, i) for i in range(n_tm)])  5.02 us
  transfers between devices with their start and end apart: 2, of which 0 were waited for; matrix products, arithmetic and copies ran while one was open for 4% of the time, Pallas kernels for 0%

commit v1 on v0

--- a/solution.py
+++ b/solution.py
@@ -1,3 +1,4 @@
+import functools
 import math
 
 import jax
@@ -28,38 +29,9 @@
     return jnp.where(inside, values, 0.0).astype(jnp.bfloat16)
 
 
-def spread_kernel(s_ref, h_ref, w_ref, e_ref, o_ref):
-    rows = s_ref.shape[0] * s_ref.shape[1] * s_ref.shape[2]
-    s = s_ref[...].reshape(rows, s_ref.shape[3])
-    h = h_ref[...].reshape(rows, h_ref.shape[3])
-    acc = jnp.dot(s, w_ref[...], preferred_element_type=jnp.float32)
-    acc = acc + jnp.dot(h, e_ref[...], preferred_element_type=jnp.float32)
-    acc = acc.astype(jnp.bfloat16)
-    for j in range(SLABS):
-        o_ref[0, j] = acc[:, j * FFT_HI : (j + 1) * FFT_HI]
-
-
-def spread(strengths, halo_cols, table, select, n_tm):
-    parts, groups, channels, samples = strengths.shape
-    chunk = channels // n_tm
-    rows = parts * groups * chunk
-    lanes = halo_cols.shape[3]
-    return pl.pallas_call(
-        spread_kernel,
-        out_shape=jax.ShapeDtypeStruct((n_tm, SLABS, rows, FFT_HI), jnp.bfloat16),
-        grid=(n_tm,),
-        in_specs=[
-            pl.BlockSpec((parts, groups, chunk, samples), lambda d: (0, 0, d, 0)),
-            pl.BlockSpec((parts, groups, chunk, lanes), lambda d: (0, 0, d, 0)),
-            pl.BlockSpec((samples, GRID_DEV), lambda d: (0, 0)),
-            pl.BlockSpec((lanes, GRID_DEV), lambda d: (0, 0)),
-        ],
-        out_specs=pl.BlockSpec((1, SLABS, rows, FFT_HI), lambda d: (d, 0, 0, 0)),
-        name="spread",
-    )(strengths, halo_cols, table, select)
-
-
-def exchange_kernel(n_tm, n_fq, src, out, send1, recv1, send2, recv2, local_sem):
+def exchange_kernel(
+    n_tm, n_fq, strengths, halo, table, select, out, held, src, load, send1, recv1, send2, recv2, local_sem
+):
     t = lax.axis_index("tm")
     f = lax.axis_index("freq")
     span = n_tm // n_fq
@@ -77,6 +49,37 @@
 
     lax.fori_loop(1, n_tm, greet_tm, 0)
     lax.fori_loop(1, n_fq, greet_fq, 0)
+    half = n_tm // 2
+    upper = lax.div(t, half)
+    chunk = held.shape[3]
+    rows = src.shape[2]
+
+    def dest(i):
+        side = jnp.where(i < half, 1 - upper, upper)
+        return side * half + lax.rem(t + 1 + i, half)
+
+    def fetch(i):
+        channels = pl.ds(pl.multiple_of(dest(i) * chunk, chunk), chunk)
+        return pltpu.make_async_copy(strengths.at[:, :, channels, :], held.at[i], load.at[i])
+
+    def fetch_one(i, c):
+        fetch(i).start()
+        return c
+
+    lax.fori_loop(0, n_tm, fetch_one, 0)
+
+    def make(i):
+        fetch(i).wait()
+        channels = pl.ds(pl.multiple_of(dest(i) * chunk, chunk), chunk)
+        x = held[i].reshape(rows, held.shape[4])
+        h = halo[:, :, channels, :].reshape(rows, halo.shape[3])
+        acc = jnp.dot(x, table[...], preferred_element_type=jnp.float32)
+        acc = acc + jnp.dot(h, select[...], preferred_element_type=jnp.float32)
+        acc = acc.astype(jnp.bfloat16)
+        for j in range(SLABS):
+            src[dest(i), j] = acc[:, j * FFT_HI : (j + 1) * FFT_HI]
+
+    make(0)
     pl.semaphore_wait(barrier, n_tm - 1 + n_fq - 1)
 
     def place(target):
@@ -122,19 +125,12 @@
             device_id_type=MESH,
         )
 
-    half = n_tm // 2
-    upper = lax.div(t, half)
-
-    def far(i, c):
-        first((1 - upper) * half + lax.rem(t + i, half)).start()
-        return c
-
-    def near(i, c):
-        first(upper * half + lax.rem(t + i, half)).start()
-        return c
-
-    lax.fori_loop(0, half, far, 0)
-    lax.fori_loop(1, half, near, 0)
+    def step(i, c):
+        make(i)
+        first(dest(i - 1)).start()
+        return c
+
+    lax.fori_loop(1, n_tm, step, 0)
     own = pltpu.make_async_copy(src.at[t], out.at[place(home), slot], local_sem)
     own.start()
     own.wait()
@@ -143,7 +139,7 @@
         target = lax.rem(f + k, n_fq)
 
         def relay(i, c):
-            s = lax.rem(slot + span - i, span)
+            s = lax.rem(slot + 2 * span - 1 - i, span)
             origin = target * span + s
 
             @pl.when(origin != t)
@@ -187,25 +183,31 @@
     lax.fori_loop(1, n_fq, finish_group, 0)
 
 
-def exchange(blocks, n_tm, n_fq):
-    import functools
-
+def exchange(strengths, halo_cols, table, select, n_tm, n_fq):
+    parts, groups, channels, samples = strengths.shape
     span = n_tm // n_fq
+    chunk = channels // n_tm
+    block = (SLABS, parts * groups * chunk, FFT_HI)
     return pl.pallas_call(
         functools.partial(exchange_kernel, n_tm, n_fq),
-        out_shape=jax.ShapeDtypeStruct((2 * n_fq, span) + blocks.shape[1:], jnp.bfloat16),
-        in_specs=[pl.BlockSpec(memory_space=pl.ANY)],
+        out_shape=jax.ShapeDtypeStruct((2 * n_fq, span) + block, jnp.bfloat16),
+        in_specs=[pl.BlockSpec(memory_space=pl.ANY)] + [pl.BlockSpec(memory_space=pltpu.VMEM)] * 3,
         out_specs=pl.BlockSpec(memory_space=pl.ANY),
         scratch_shapes=[
+            pltpu.VMEM((n_tm, parts, groups, chunk, samples), jnp.bfloat16),
+            pltpu.VMEM((n_tm,) + block, jnp.bfloat16),
+            pltpu.SemaphoreType.DMA((n_tm,)),
             pltpu.SemaphoreType.DMA((n_tm,)),
             pltpu.SemaphoreType.DMA((n_tm,)),
             pltpu.SemaphoreType.DMA((n_fq, span)),
             pltpu.SemaphoreType.DMA((n_fq, span)),
             pltpu.SemaphoreType.DMA,
         ],
-        compiler_params=pltpu.CompilerParams(collective_id=0, has_side_effects=True),
-        name="exchange",
-    )(blocks)
+        compiler_params=pltpu.CompilerParams(
+            collective_id=0, has_side_effects=True, vmem_limit_bytes=48 * 1024 * 1024
+        ),
+        name="spread_exchange",
+    )(strengths, halo_cols, table, select)
 
 
 def fft_list(re, im):
@@ -233,7 +235,7 @@
     return out_r, out_i
 
 
-def transform_kernel(x_ref, tc_ref, ts_ref, hi_ref, lo_ref, o_ref, lhs, turned):
+def transform_kernel(x_ref, tc_ref, ts_ref, hi_ref, o_ref, lhs):
     chunk = x_ref.shape[5]
     re = [x_ref[0, n // SLABS, n % SLABS, 0, 0].astype(jnp.float32) for n in range(FFT_LO)]
     im = [x_ref[0, n // SLABS, n % SLABS, 1, 0].astype(jnp.float32) for n in range(FFT_LO)]
@@ -246,13 +248,12 @@
         lhs[rows, FFT_HI:] = (im[a] * c - re[a] * s).astype(jnp.bfloat16)
     x = lhs[...]
     y = jnp.dot(x, hi_ref[...], preferred_element_type=jnp.float32)
-    y = y + jnp.dot(x, lo_ref[...], preferred_element_type=jnp.float32)
-    for p in range(2):
-        for a in range(FFT_LO):
-            turned[p, pl.ds(a, chunk, stride=FFT_LO), :] = y[
+    flat = o_ref.reshape(2, chunk * FFT_LO, FFT_HI)
+    for a in range(FFT_LO):
+        for p in range(2):
+            flat[p, pl.ds(a, chunk, stride=FFT_LO), :] = y[
                 a * chunk : (a + 1) * chunk, p * FFT_HI : (p + 1) * FFT_HI
             ]
-        o_ref[p, 0, :, 0] = turned[p].reshape(chunk, FFT_LO, FFT_HI)
 
 
 def transform(held, n_fq, groups, chunk, frames):
@@ -263,7 +264,6 @@
     hc, hs = np.cos(high), np.sin(high)
     full = np.block([[hc, -hs], [hs, hc]]).astype(np.float32) / math.sqrt(FFTLEN)
     hi = full.astype(jnp.bfloat16)
-    lo = (full - hi.astype(np.float32)).astype(jnp.bfloat16)
     whole = lambda shape: pl.BlockSpec(shape, lambda f, g, m: (0, 0))
     return pl.pallas_call(
         transform_kernel,
@@ -278,14 +278,12 @@
             whole((FFT_LO, FFT_HI)),
             whole((FFT_LO, FFT_HI)),
             whole((2 * FFT_HI, 2 * FFT_HI)),
-            whole((2 * FFT_HI, 2 * FFT_HI)),
         ],
         out_specs=pl.BlockSpec(
             (2, 1, chunk, 1, FFT_LO, FFT_HI), lambda f, g, m: (0, f * groups + g, 0, m, 0, 0)
         ),
         scratch_shapes=[
             pltpu.VMEM((FFT_LO * chunk, 2 * FFT_HI), jnp.bfloat16),
-            pltpu.VMEM((2, FFT_LO * chunk, FFT_HI), jnp.float32),
         ],
         name="transform",
     )(
@@ -293,7 +291,6 @@
         jnp.asarray(np.cos(low), jnp.float32),
         jnp.asarray(np.sin(low), jnp.float32),
         jnp.asarray(hi),
-        jnp.asarray(lo),
     )
 
 
@@ -328,14 +325,14 @@
         for k in range(HALF):
             pick[r * TAPS + k, k] = 1.0
             pick[r * TAPS + HALF + k, GRID_DEV - HALF + k] = 1.0
-    blocks = spread(
+    held = exchange(
         strengths,
         halo_cols.reshape(parts, groups, channels, 128),
         table,
         jnp.asarray(pick, jnp.bfloat16),
         n_tm,
-    )
-    held = exchange(blocks, n_tm, n_fq)
+        n_fq,
+    )
     frames = n_tm // PER_FRAME // n_fq
     return transform(held, n_fq, groups, channels // n_tm, frames)
 

time: 162 us -> 146 us (0.901)
  Pallas kernels: 142 us -> 123 us
    pallas_call x1 -> x0, Pallas kernels: 18.5 us -> none  [spread(): pl.pallas_call(spread_kernel, out_shape=jax.ShapeDtypeStruct((n_tm, SLABS...]
    unnamed x3 -> x7, local copies, waits for them, and re-layouts: 0.28 us -> 2.46 us
where the time goes in v1:
time: 146 us; the launch traced here: 144 us
  Pallas kernels  123 us (84%)
  other arithmetic  6.95 us (5%)
  matrix products  5.67 us (4%)
  starting transfers between devices  5.57 us (4%)
  local copies, waits for them, and re-layouts  2.6 us (2%)
    pallas_call x1, Pallas kernels, exchange(): pl.pallas_call(functools.partial(exchange_kernel, n_tm, n_fq), out_shape=...  106 us
    pallas_call x1, Pallas kernels, transform(): pl.pallas_call(transform_kernel, out_shape=jax.ShapeDtypeStruct((2, n_fq...  17 us
    convert_element_type x1, other arithmetic, tap_table(): return jnp.where(inside, values, 0.0).astype(jnp.bfloat16)  6.13 us
    dot_general x1, matrix products, shards(): lax.dot_general(edge_table, strengths.reshape(parts * groups * channels,...  5.67 us
    ppermute x1, starting transfers between devices, shards(): lax.ppermute(edges[:HALF], 'tm', [((i + 1) % n_tm, i) for i in range(n_tm)])  5.02 us
  transfers between devices with their start and end apart: 2, of which 0 were waited for; matrix products, arithmetic and copies ran while one was open for 4% of the time, Pallas kernels for 0%

profile of v1, /device:TPU:0, one launch (start us, length us, event | category | flops | bytes accessed | tf_op | source)
XLA Modules:
  0.0 143.7 jit_solution(16430014768831490943)
XLA Ops:
  0.0 0.0 copy-start.1
  0.0 0.0 copy-start.2
  0.0 0.1 pad_add_fusion
  0.1 0.7 broadcast_subtract_fusion
  0.8 5.7 %fusion.7 = f32[8,2048]{1,0:T(8,128)S(1)} fusion(bf16[2048,2048]{1,0:T(8,128)(2,1)} %bitcast.7, f32[2048]{0:T(1024)} %param.9, s32[2048]{0:T(1024)S(1)} %broadcast_subtract_fusion, s32[8]{0:T(128)S(1)} %pad_add_fusion), kind=kOutput, calls=%fused_computation.17 | convolution fusion | flops 67305472 | bytes 8470560 | tf_op jit(solution)/shard_map/dot_general | solution.py:308
  6.5 0.6 collective-permute-start
  7.0 5.0 %collective-permute-start.1 = (f32[4,2048]{1,0:T(4,128)S(1)}, f32[4,2048]{1,0:T(4,128)S(1)}, u32[]{:S(2)}, u32[]{:S(2)}) collective-permute-start(f32[4,2048]{1,0:T(4,128)S(1)} %get-tuple-element.9), channel_id=1, source_target_pairs={{2,0},{4,2},{6,4},{8,6},{10,8},{12,10},{14,12},{16,14},{18,16},{20... | collective-permute-start | bytes 98312 | tf_op jit(solution)/shard_map/ppermute | solution.py:315
  12.1 0.0 copy-done.2
  12.1 6.1 %select_convert_fusion.table = bf16[2048,1024]{1,0:T(8,128)(2,1)} fusion(f32[2048]{0:T(1024)S(1)} %copy-done.2, s32[2048]{0:T(1024)S(1)} %broadcast_subtract_fusion, s32[1024]{0:T(1024)S(1)} %iota_add_fusion), kind=kLoop, calls=%fused_computation | loop fusion | flops 25165824 | bytes 4214784 | tf_op jit(solution)/shard_map/convert_element_type | solution.py:29
  18.2 0.0 collective-permute-done
  18.2 0.0 collective-permute-done.1
  18.3 0.3 copy.10
  18.5 0.1 pad.5.clone
  18.7 0.0 copy-done.1
  18.7 0.0 copy-start
  18.7 2.2 %copy-done = bf16[2048,1024]{1,0:T(8,128)(2,1)S(1)} copy-done((bf16[2048,1024]{1,0:T(8,128)(2,1)S(1)}, bf16[2048,1024]{1,0:T(8,128)(2,1)}, u32[]{:S(2)}) %copy-start) | copy-done | bytes 4194328
  20.9 105.9 %spread_exchange.1 = bf16[4,8,8,128,128]{4,3,2,1,0:T(8,128)(2,1)} custom-call(bf16[2,4,256,2048]{3,2,1,0:T(8,128)(2,1)} %strengths.1, bf16[2,4,256,128]{3,2,1,0:T(8,128)(2,1)S(1)} %bitcast.6, bf16[2048,1024]{1,0:T(8,128)(2,1)S(1)} %copy-done, bf16[128,1024]{1,0:T(8,128)(2,1)S(1)} %copy-done.1), custom_call_target="tpu_custom_call" | custom-call | tf_op jit(solution)/shard_map/spread_exchange/pallas_call | solution.py:191
  126.8 17.0 %transform.1 = f32[2,8,16,2,32,128]{5,4,3,2,1,0:T(8,128)} custom-call(bf16[4,8,8,2,4,16,128]{6,5,4,3,2,1,0:T(8,128)(2,1)} %bitcast.8, f32[32,128]{1,0:T(8,128)} %constant.46.clone.tc_ref, f32[32,128]{1,0:T(8,128)} %constant.47.clone.ts_ref, bf16[256,256]{1,0:T(8,128)(2,1)} %constant.48.clone.hi_ref), custom_call_target="tpu_custom_call" | custom-call | tf_op jit(solution)/shard_map/transform/pallas_call | solution.py:268
  (6 shorter events, 0.1 us)
Async XLA Ops:
  0.0 18.7 %copy-start.1 = (bf16[128,1024]{1,0:T(8,128)(2,1)S(1)}, bf16[128,1024]{1,0:T(8,128)(2,1)}, u32[]{:S(2)}) copy-start(bf16[128,1024]{1,0:T(8,128)(2,1)} %constant.45.clone.select) | copy-start | bytes 786436
  0.0 12.1 %copy-start.2 = (f32[2048]{0:T(1024)S(1)}, f32[2048]{0:T(1024)}, u32[]{:S(2)}) copy-start(f32[2048]{0:T(1024)} %param.9) | copy-start | bytes 24580
  6.5 11.7 %collective-permute-start = (f32[4,2048]{1,0:T(4,128)S(1)}, f32[4,2048]{1,0:T(4,128)S(1)}, u32[]{:S(2)}, u32[]{:S(2)}) collective-permute-start(f32[4,2048]{1,0:T(4,128)S(1)} %get-tuple-element.8), channel_id=1, source_target_pairs={{0,2},{2,4},{4,6},{6,8},{8,10},{10,12},{12,14},{14,16},{16,18},{18... | collective-permute-start | bytes 98312 | tf_op jit(solution)/shard_map/ppermute | solution.py:314
  7.0 11.2 %collective-permute-start.1 = (f32[4,2048]{1,0:T(4,128)S(1)}, f32[4,2048]{1,0:T(4,128)S(1)}, u32[]{:S(2)}, u32[]{:S(2)}) collective-permute-start(f32[4,2048]{1,0:T(4,128)S(1)} %get-tuple-element.9), channel_id=1, source_target_pairs={{2,0},{4,2},{6,4},{8,6},{10,8},{12,10},{14,12},{16,14},{18,16},{20... | collective-permute-start | bytes 98312 | tf_op jit(solution)/shard_map/ppermute | solution.py:315
  18.7 2.2 %copy-start = (bf16[2048,1024]{1,0:T(8,128)(2,1)S(1)}, bf16[2048,1024]{1,0:T(8,128)(2,1)}, u32[]{:S(2)}) copy-start(bf16[2048,1024]{1,0:T(8,128)(2,1)} %select_convert_fusion.table) | copy-start | bytes 12582916

commit v2 on v1

--- a/solution.py
+++ b/solution.py
@@ -51,12 +51,14 @@
     lax.fori_loop(1, n_fq, greet_fq, 0)
     half = n_tm // 2
     upper = lax.div(t, half)
+    quarter = lax.div(t, half // 2)
+    outer = lax.rem(lax.div(quarter + 1, 2) + 1, 2)
     chunk = held.shape[3]
     rows = src.shape[2]
 
     def dest(i):
-        side = jnp.where(i < half, 1 - upper, upper)
-        return side * half + lax.rem(t + 1 + i, half)
+        side = lax.rem(lax.div(i, half) + 1 + outer + upper, 2)
+        return side * half + lax.rem(t + half // 2 + i, half)
 
     def fetch(i):
         channels = pl.ds(pl.multiple_of(dest(i) * chunk, chunk), chunk)
@@ -127,19 +129,28 @@
 
     def step(i, c):
         make(i)
-        first(dest(i - 1)).start()
-        return c
+        send(i - 1)
+        return c
+
+    def send(i):
+        peer = dest(i)
+
+        @pl.when(peer != t)
+        def _():
+            first(peer).start()
 
     lax.fori_loop(1, n_tm, step, 0)
     own = pltpu.make_async_copy(src.at[t], out.at[place(home), slot], local_sem)
     own.start()
     own.wait()
+    send(n_tm - 1)
 
     def relay_group(k, c):
         target = lax.rem(f + k, n_fq)
 
         def relay(i, c):
-            s = lax.rem(slot + 2 * span - 1 - i, span)
+            part = span // 2
+            s = lax.rem(lax.div(i, part) + upper, 2) * part + lax.rem(slot + 2 * span - i, part)
             origin = target * span + s
 
             @pl.when(origin != t)

time: 146 us -> 165 us (1.13)
  Pallas kernels: 123 us -> 143 us
    pallas_call x1, Pallas kernels: 106 us -> 126 us  [exchange(): pl.pallas_call(functools.partial(exchange_kernel, n_tm, n_fq), out_shape=...]
where the time goes in v2:
time: 165 us; the launch traced here: 164 us
  Pallas kernels  143 us (87%)
  other arithmetic  6.95 us (4%)
  matrix products  5.67 us (3%)
  starting transfers between devices  5.57 us (3%)
  local copies, waits for them, and re-layouts  2.6 us (2%)
    pallas_call x1, Pallas kernels, exchange(): pl.pallas_call(functools.partial(exchange_kernel, n_tm, n_fq), out_shape=...  126 us
    pallas_call x1, Pallas kernels, transform(): pl.pallas_call(transform_kernel, out_shape=jax.ShapeDtypeStruct((2, n_fq...  17 us
    convert_element_type x1, other arithmetic, tap_table(): return jnp.where(inside, values, 0.0).astype(jnp.bfloat16)  6.13 us
    dot_general x1, matrix products, shards(): lax.dot_general(edge_table, strengths.reshape(parts * groups * channels,...  5.67 us
    ppermute x1, starting transfers between devices, shards(): lax.ppermute(edges[:HALF], 'tm', [((i + 1) % n_tm, i) for i in range(n_tm)])  5.02 us
  transfers between devices with their start and end apart: 2, of which 0 were waited for; matrix products, arithmetic and copies ran while one was open for 4% of the time, Pallas kernels for 0%

profile of v2, /device:TPU:0, one launch (start us, length us, event | category | flops | bytes accessed | tf_op | source)
XLA Modules:
  0.0 163.6 jit_solution(10036405229166052180)
XLA Ops:
  0.0 0.0 copy-start.1
  0.0 0.0 copy-start.2
  0.0 0.1 pad_add_fusion
  0.1 0.7 broadcast_subtract_fusion
  0.8 5.7 %fusion.7 = f32[8,2048]{1,0:T(8,128)S(1)} fusion(bf16[2048,2048]{1,0:T(8,128)(2,1)} %bitcast.7, f32[2048]{0:T(1024)} %param.9, s32[2048]{0:T(1024)S(1)} %broadcast_subtract_fusion, s32[8]{0:T(128)S(1)} %pad_add_fusion), kind=kOutput, calls=%fused_computation.17 | convolution fusion | flops 67305472 | bytes 8470560 | tf_op jit(solution)/shard_map/dot_general | solution.py:319
  6.5 0.6 collective-permute-start
  7.0 5.0 %collective-permute-start.1 = (f32[4,2048]{1,0:T(4,128)S(1)}, f32[4,2048]{1,0:T(4,128)S(1)}, u32[]{:S(2)}, u32[]{:S(2)}) collective-permute-start(f32[4,2048]{1,0:T(4,128)S(1)} %get-tuple-element.9), channel_id=1, source_target_pairs={{2,0},{4,2},{6,4},{8,6},{10,8},{12,10},{14,12},{16,14},{18,16},{20... | collective-permute-start | bytes 98312 | tf_op jit(solution)/shard_map/ppermute | solution.py:326
  12.1 0.0 copy-done.2
  12.1 6.1 %select_convert_fusion.table = bf16[2048,1024]{1,0:T(8,128)(2,1)} fusion(f32[2048]{0:T(1024)S(1)} %copy-done.2, s32[2048]{0:T(1024)S(1)} %broadcast_subtract_fusion, s32[1024]{0:T(1024)S(1)} %iota_add_fusion), kind=kLoop, calls=%fused_computation | loop fusion | flops 25165824 | bytes 4214784 | tf_op jit(solution)/shard_map/convert_element_type | solution.py:29
  18.2 0.0 collective-permute-done
  18.2 0.0 collective-permute-done.1
  18.3 0.3 copy.10
  18.5 0.1 pad.5.clone
  18.7 0.0 copy-done.1
  18.7 0.0 copy-start
  18.7 2.2 %copy-done = bf16[2048,1024]{1,0:T(8,128)(2,1)S(1)} copy-done((bf16[2048,1024]{1,0:T(8,128)(2,1)S(1)}, bf16[2048,1024]{1,0:T(8,128)(2,1)}, u32[]{:S(2)}) %copy-start) | copy-done | bytes 4194328
  20.9 125.8 %spread_exchange.1 = bf16[4,8,8,128,128]{4,3,2,1,0:T(8,128)(2,1)} custom-call(bf16[2,4,256,2048]{3,2,1,0:T(8,128)(2,1)} %strengths.1, bf16[2,4,256,128]{3,2,1,0:T(8,128)(2,1)S(1)} %bitcast.6, bf16[2048,1024]{1,0:T(8,128)(2,1)S(1)} %copy-done, bf16[128,1024]{1,0:T(8,128)(2,1)S(1)} %copy-done.1), custom_call_target="tpu_custom_call" | custom-call | tf_op jit(solution)/shard_map/spread_exchange/pallas_call | solution.py:202
  146.6 17.0 %transform.1 = f32[2,8,16,2,32,128]{5,4,3,2,1,0:T(8,128)} custom-call(bf16[4,8,8,2,4,16,128]{6,5,4,3,2,1,0:T(8,128)(2,1)} %bitcast.8, f32[32,128]{1,0:T(8,128)} %constant.46.clone.tc_ref, f32[32,128]{1,0:T(8,128)} %constant.47.clone.ts_ref, bf16[256,256]{1,0:T(8,128)(2,1)} %constant.48.clone.hi_ref), custom_call_target="tpu_custom_call" | custom-call | tf_op jit(solution)/shard_map/transform/pallas_call | solution.py:279
  (6 shorter events, 0.1 us)
Async XLA Ops:
  0.0 18.7 %copy-start.1 = (bf16[128,1024]{1,0:T(8,128)(2,1)S(1)}, bf16[128,1024]{1,0:T(8,128)(2,1)}, u32[]{:S(2)}) copy-start(bf16[128,1024]{1,0:T(8,128)(2,1)} %constant.45.clone.select) | copy-start | bytes 786436
  0.0 12.1 %copy-start.2 = (f32[2048]{0:T(1024)S(1)}, f32[2048]{0:T(1024)}, u32[]{:S(2)}) copy-start(f32[2048]{0:T(1024)} %param.9) | copy-start | bytes 24580
  6.5 11.7 %collective-permute-start = (f32[4,2048]{1,0:T(4,128)S(1)}, f32[4,2048]{1,0:T(4,128)S(1)}, u32[]{:S(2)}, u32[]{:S(2)}) collective-permute-start(f32[4,2048]{1,0:T(4,128)S(1)} %get-tuple-element.8), channel_id=1, source_target_pairs={{0,2},{2,4},{4,6},{6,8},{8,10},{10,12},{12,14},{14,16},{16,18},{18... | collective-permute-start | bytes 98312 | tf_op jit(solution)/shard_map/ppermute | solution.py:325
  7.0 11.2 %collective-permute-start.1 = (f32[4,2048]{1,0:T(4,128)S(1)}, f32[4,2048]{1,0:T(4,128)S(1)}, u32[]{:S(2)}, u32[]{:S(2)}) collective-permute-start(f32[4,2048]{1,0:T(4,128)S(1)} %get-tuple-element.9), channel_id=1, source_target_pairs={{2,0},{4,2},{6,4},{8,6},{10,8},{12,10},{14,12},{16,14},{18,16},{20... | collective-permute-start | bytes 98312 | tf_op jit(solution)/shard_map/ppermute | solution.py:326
  18.7 2.2 %copy-start = (bf16[2048,1024]{1,0:T(8,128)(2,1)S(1)}, bf16[2048,1024]{1,0:T(8,128)(2,1)}, u32[]{:S(2)}) copy-start(bf16[2048,1024]{1,0:T(8,128)(2,1)} %select_convert_fusion.table) | copy-start | bytes 12582916
